TPU v7x, 32 devices: a whole 2x2x4 slice. The times are simulated.
32 devices in a mesh: group: 2 (over y), seq: 4 (over z), tensor: 4 (over x, core).
Axes of the slice: x: 2, y: 2, z: 4, core: 2. Of those that a mesh axis runs over, the one named last changes fastest.
Arguments:
- query: bfloat16 [16, 7168], P(('group', 'seq'), 'tensor'), parts along dimension 0, may hold values from -5 to 5
- key_cache: bfloat16 [32, 256, 7168], P(('group', 'seq'), None, 'tensor'), parts along dimension 0, may hold values from -5 to 5
- value_cache: bfloat16 [32, 256, 7168], P(('group', 'seq'), None, 'tensor'), parts along dimension 0, may hold values from -6 to 6
- alibi_slopes: float32 [56], P('tensor'), may hold values from 0 to 1, as said below
- block_seq: int32 [32], P(('group', 'seq')), parts along dimension 0, may hold values from 0 to 7, as said below
- block_pos: int32 [32], P(('group', 'seq')), parts along dimension 0, may hold values from 0 to 2, as said below
- lengths: int32 [16], P('group'), parts along dimension 0, may hold values from 1 to 768, as said below
- out_weight: bfloat16 [7168, 14336], P('tensor', 'seq'), may hold values from -0.5 to 0.5
Outputs:
- mixed: bfloat16 [16, 14336], P(('group', 'tensor'), 'seq'), parts along dimension 0
There are 2 independent parts, one for each index of `group`. A program takes and returns all parts, laid end to end along the dimension named above; an argument that names none is the same for every part. Nothing has to cross between parts.
Inputs may be any that keep to these rules, and one draw needn't show every extreme that they name: `block_seq`: every sequence owns at least one block and at most 3; the blocks of sequence s have block_pos 0 to n_s - 1, each once. block_pos of a block is below the number of blocks its sequence owns. `lengths`: A sequence that owns n blocks has a length above 256 * (n - 1) and at most 256 * n. `alibi_slopes`: positive slopes.
All inputs are finite; a program needn't handle non-finite values.
Results may differ from a plain program's by a relative error of at most 0.0054.
Values may be sent and summed in bfloat16 or wider, within the bound.
No kernel may reach another device: no remote copies, remote signals or barrier semaphores. Data moves between devices by JAX's collectives and lax.ppermute only.
A program may use at most 64 MiB of HBM per device.

v0:
```python
import math
import jax
import jax.numpy as jnp
from jax import lax
from jax.sharding import PartitionSpec as P


def local(query, key_cache, value_cache, alibi_slopes, block_seq, block_pos, lengths, out_weight):
    heads = alibi_slopes.shape[0]
    features = query.shape[1]
    head_size = features // heads
    blocks_here = key_cache.shape[0]
    block_len = key_cache.shape[1]
    seq_count = lengths.shape[0]
    scale = 1.0 / math.sqrt(head_size)
    whole_query = lax.all_gather(query, "seq", axis=0, tiled=True)
    query_rows = jnp.take(whole_query, block_seq, axis=0).reshape(blocks_here, heads, head_size)
    keys = key_cache.reshape(blocks_here, block_len, heads, head_size)
    values = value_cache.reshape(blocks_here, block_len, heads, head_size)
    scores = (
        jnp.einsum("bthd,bhd->bht", keys, query_rows, preferred_element_type=jnp.float32) * scale
    )
    owner_length = lengths[block_seq]
    placed = block_pos[:, None] * block_len + jnp.arange(block_len, dtype=jnp.int32)[None, :]
    live = (placed < owner_length[:, None])[:, None, :]
    distance = (owner_length[:, None] - 1 - placed).astype(jnp.float32)
    scores = scores - alibi_slopes[None, :, None] * distance[:, None, :]
    scores = jnp.where(live, scores, -1e30)
    block_top = jnp.max(scores, axis=2)
    weights = jnp.where(live, jnp.exp(scores - block_top[:, :, None]), 0.0)
    block_total = jnp.sum(weights, axis=2)
    block_acc = jnp.einsum(
        "bht,bthd->bhd", weights.astype(jnp.bfloat16), values, preferred_element_type=jnp.float32
    )
    seq_ids = jnp.arange(seq_count, dtype=jnp.int32)
    owned = (block_seq[None, :] == seq_ids[:, None])[:, :, None]
    local_top = jnp.max(jnp.where(owned, block_top[None], -1e30), axis=1)
    factor = jnp.where(owned, jnp.exp(block_top[None] - local_top[:, None, :]), 0.0)
    local_total = jnp.sum(factor * block_total[None], axis=1)
    local_acc = jnp.einsum("sbh,bhd->shd", factor, block_acc, precision=lax.Precision.HIGHEST)
    tops, totals, accs = (
        lax.all_to_all(local_top[None], "seq", split_axis=1, concat_axis=0, tiled=True),
        lax.all_to_all(local_total[None], "seq", split_axis=1, concat_axis=0, tiled=True),
        lax.all_to_all(local_acc[None], "seq", split_axis=1, concat_axis=0, tiled=True),
    )
    best = jnp.max(tops, axis=0)
    scaling = jnp.exp(tops - best[None])
    home_total = jnp.sum(totals * scaling, axis=0)
    home_acc = jnp.sum(accs * scaling[..., None], axis=0)
    mine = (
        (home_acc / home_total[:, :, None])
        .astype(jnp.bfloat16)
        .reshape(home_acc.shape[0], features)
    )
    attention = lax.all_gather(mine, "seq", axis=0, tiled=True)
    mixed = lax.psum_scatter(
        jnp.dot(attention, out_weight, preferred_element_type=jnp.float32),
        "tensor",
        scatter_dimension=0,
        tiled=True,
    )
    return mixed.astype(jnp.bfloat16)


def solution(mesh):
    placed = (
        P(("group", "seq"), "tensor"),
        P(("group", "seq"), None, "tensor"),
        P(("group", "seq"), None, "tensor"),
        P("tensor"),
        P(("group", "seq")),
        P(("group", "seq")),
        P("group"),
        P("tensor", "seq"),
    )
    return jax.shard_map(
        local, mesh=mesh, in_specs=placed, out_specs=P(("group", "tensor"), "seq"), check_vma=False
    )
```

profile of v0, /device:TPU:0, one launch (start us, length us, event | category | flops | bytes accessed | tf_op | source)
XLA Modules:
  0.0 95.4 jit_solution(14486349411866468453)
XLA Ops:
  0.0 0.7 compare_select_fusion
  0.7 0.7 compare_and_fusion
  1.3 0.7 iota_compare_fusion
  2.1 0.6 gather_fusion
  2.7 0.7 broadcast_add_fusion
  3.5 15.1 %all-gather = bf16[4,2,1792]{2,1,0:T(2,128)(2,1)S(1)} all-gather(bf16[1,2,1792]{2,1,0:T(2,128)(2,1)} %bitcast.41), channel_id=1, replica_groups=mesh['group'=2,'seq'=4,'tensor'=4] {'seq'}, dimensions={0}, use_global_device_ids=true | all-gather | bytes 35840 | tf_op jit(solution)/shard_map/all_gather | solution.py:16
  18.6 0.6 gather_fusion.1
  19.2 6.0 %copy.49 = bf16[4,256,1792]{1,2,0:T(8,128)(2,1)} copy(bf16[4,256,1792]{2,1,0:T(8,128)(2,1)} %param.9) | data formatting | bytes 7340032 | tf_op args[1]
  25.3 2.6 %fusion.9 = f32[4,14,1,256]{3,2,1,0:T(1,128)S(1)} fusion(bf16[4,256,14,128]{1,3,2,0:T(8,128)(2,1)} %bitcast.33, bf16[4,14,128,1]{2,1,0,3:T(8,128)(2,1)S(1)} %select_bitcast_fusion), kind=kOutput, calls=%fused_computation.16 | convolution fusion | flops 3670016 | bytes 3741696 | tf_op jit(solution)/shard_map/bthd,bhd->bht/dot_general | solution.py:21
  28.1 0.7 copy.54
  28.8 4.7 %all-to-all-start.1 = ((f32[1,8,14]{2,0,1:T(1,128)}), f32[1,8,14]{2,0,1:T(1,128)S(1)}, u32[]{:S(2)}, u32[]{:S(2)}) async-start(f32[1,8,14]{2,0,1:T(1,128)} %copy.54), calls=%async_computation.1 | async-start | bytes 8192 | tf_op jit(solution)/shard_map/all_to_all | solution.py:42
  33.8 6.0 %copy.50 = bf16[4,256,1792]{1,2,0:T(8,128)(2,1)} copy(bf16[4,256,1792]{2,1,0:T(8,128)(2,1)} %param.10) | data formatting | bytes 7340032 | tf_op args[2]
  39.8 3.1 %fusion.2 = f32[4,14,1,128]{3,2,1,0:T(1,128)S(1)} fusion(bf16[4,256,14,128]{1,3,2,0:T(8,128)(2,1)} %bitcast.34, bf16[4,14,256,1]{2,0,1,3:T(4,128)(2,1)S(1)} %get-tuple-element.10), kind=kOutput, calls=%fused_computation.6 | convolution fusion | flops 3670016 | bytes 3727360 | tf_op jit(solution)/shard_map/bht,bthd->bhd/dot_general | solution.py:32
  43.3 0.7 copy.57
  44.0 5.1 %all-to-all-start.2 = ((f32[1,8,14]{2,0,1:T(1,128)}), f32[1,8,14]{2,0,1:T(1,128)S(1)}, u32[]{:S(2)}, u32[]{:S(2)}) async-start(f32[1,8,14]{2,0,1:T(1,128)} %copy.57), calls=%async_computation.2 | async-start | bytes 8192 | tf_op jit(solution)/shard_map/all_to_all | solution.py:43
  49.1 0.7 copy.51
  49.7 0.6 dynamic-slice
  51.0 3.7 %all-to-all-done.2 = f32[1,8,14]{2,0,1:T(1,128)S(1)} async-done(((f32[1,8,14]{2,0,1:T(1,128)}), f32[1,8,14]{2,0,1:T(1,128)S(1)}, u32[]{:S(2)}, u32[]{:S(2)}) %all-to-all-start.2) | async-done | bytes 480 | tf_op jit(solution)/shard_map/all_to_all | solution.py:43
  54.6 3.3 %all-to-all-start = ((f32[1,8,14,128]{3,0,2,1:T(1,128)}), f32[1,8,14,128]{3,0,2,1:T(1,128)S(1)}, u32[]{:S(2)}, u32[]{:S(2)}) async-start(f32[1,8,14,128]{3,0,2,1:T(1,128)} %copy.51), calls=%async_computation | async-start | bytes 114688 | tf_op jit(solution)/shard_map/all_to_all | solution.py:44
  58.2 5.5 %all-to-all-done = f32[1,8,14,128]{3,0,2,1:T(1,128)S(1)} async-done(((f32[1,8,14,128]{3,0,2,1:T(1,128)}), f32[1,8,14,128]{3,0,2,1:T(1,128)S(1)}, u32[]{:S(2)}, u32[]{:S(2)}) %all-to-all-start) | async-done | bytes 57376 | tf_op jit(solution)/shard_map/all_to_all | solution.py:44
  63.9 13.2 %all-gather.1 = bf16[4,2,1792]{2,1,0:T(2,128)(2,1)S(1)} all-gather(bf16[1,2,1792]{2,1,0:T(2,128)(2,1)S(1)} %fusion.15), channel_id=1, replica_groups=mesh['group'=2,'seq'=4,'tensor'=4] {'seq'}, dimensions={0}, use_global_device_ids=true | all-gather | bytes 35840 | tf_op jit(solution)/shard_map/all_gather | solution.py:55
  77.1 6.4 %fusion.20 = f32[8,3584]{1,0:T(8,128)S(1)} fusion(bf16[8,1792]{1,0:T(8,128)(2,1)S(1)} %reshape.152, bf16[1792,3584]{1,0:T(8,128)(2,1)} %param.15), kind=kOutput, calls=%fused_computation.41 | convolution fusion | flops 102760448 | bytes 12988416 | tf_op jit(solution)/shard_map/dot_general | solution.py:57
  83.5 11.3 %all-reduce = bf16[8,3584]{1,0:T(8,128)(2,1)S(1)} all-reduce(f32[8,3584]{1,0:T(8,128)S(1)} %fusion.20), channel_id=2, replica_groups=mesh['group'=2,'seq'=4,'tensor'=4] {'tensor'}, use_global_device_ids=true, to_apply=%region_7.8.clone | all-reduce | flops 28672 | bytes 172032
  94.7 0.6 dynamic-slice_convert_fusion
  (26 shorter events, 1.7 us)
Async XLA Ops:
  0.0 2.1 %copy-start = (s32[8]{0:T(128)S(1)}, s32[8]{0:T(128)}, u32[]{:S(2)}) copy-start(s32[8]{0:T(128)} %param.14) | copy-start | bytes 100
  25.2 2.7 %copy-start.1 = (f32[14]{0:T(128)S(1)}, f32[14]{0:T(128)}, u32[]{:S(2)}) copy-start(f32[14]{0:T(128)} %param.11) | copy-start | bytes 172
  28.8 15.2 %all-to-all-start.1 = ((f32[1,8,14]{2,0,1:T(1,128)}), f32[1,8,14]{2,0,1:T(1,128)S(1)}, u32[]{:S(2)}, u32[]{:S(2)}) async-start(f32[1,8,14]{2,0,1:T(1,128)} %copy.54), calls=%async_computation.1 | async-start | bytes 8192 | tf_op jit(solution)/shard_map/all_to_all | solution.py:42
  39.8 9.9 %copy-start.2 = (u32[32]{0:T(128)S(1)}, u32[32]{0:T(128)}, u32[]{:S(2)}) copy-start(u32[32]{0:T(128)} %constant.39) | copy-start | bytes 388
  44.0 10.7 %all-to-all-start.2 = ((f32[1,8,14]{2,0,1:T(1,128)}), f32[1,8,14]{2,0,1:T(1,128)S(1)}, u32[]{:S(2)}, u32[]{:S(2)}) async-start(f32[1,8,14]{2,0,1:T(1,128)} %copy.57), calls=%async_computation.2 | async-start | bytes 8192 | tf_op jit(solution)/shard_map/all_to_all | solution.py:43
  54.6 9.0 %all-to-all-start = ((f32[1,8,14,128]{3,0,2,1:T(1,128)}), f32[1,8,14,128]{3,0,2,1:T(1,128)S(1)}, u32[]{:S(2)}, u32[]{:S(2)}) async-start(f32[1,8,14,128]{3,0,2,1:T(1,128)} %copy.51), calls=%async_computation | async-start | bytes 114688 | tf_op jit(solution)/shard_map/all_to_all | solution.py:44
where the time goes:
time: 96.1 us; the launch traced here: 95.4 us
  blocking collectives  39.5 us (41%)
  local copies, waits for them, and re-layouts  16.7 us (17%)
  starting transfers between devices  13.1 us (14%)
  matrix products  12.5 us (13%)
  waiting for transfers between devices  9.12 us (9%)
  other arithmetic  3.75 us (4%)
    all_gather x1, blocking collectives, local(): whole_query = lax.all_gather(query, 'seq', axis=0, tiled=True)  15.1 us
    all_gather x1, blocking collectives, local(): attention = lax.all_gather(mine, 'seq', axis=0, tiled=True)  13.2 us
    unnamed x11, local copies, waits for them, and re-layouts  12.6 us
    unnamed x1, blocking collectives  11.3 us
    dot_general x1, matrix products, local(): jnp.dot(attention, out_weight, preferred_element_type=jnp.float32)  6.41 us
    all_to_all x1, waiting for transfers between devices, local(): lax.all_to_all(local_acc[None], 'seq', split_axis=1, concat_axis=0, tiled...  5.46 us
    all_to_all x1, starting transfers between devices, local(): lax.all_to_all(local_total[None], 'seq', split_axis=1, concat_axis=0, til...  5.09 us
    all_to_all x1, starting transfers between devices, local(): lax.all_to_all(local_top[None], 'seq', split_axis=1, concat_axis=0, tiled...  4.74 us
  transfers between devices with their start and end apart: 3, of which 2 were waited for; matrix products, arithmetic and copies ran while one was open for 13% of the time, Pallas kernels for 0%

commit v1 on v0

--- a/solution.py
+++ b/solution.py
@@ -13,7 +13,9 @@
     block_len = key_cache.shape[1]
     seq_count = lengths.shape[0]
     scale = 1.0 / math.sqrt(head_size)
-    whole_query = lax.all_gather(query, "seq", axis=0, tiled=True)
+    whole_query = jnp.concatenate(
+        lax.all_to_all(jnp.stack([query] * lax.axis_size("seq")), "seq", 0, 0), axis=0
+    )
     query_rows = jnp.take(whole_query, block_seq, axis=0).reshape(blocks_here, heads, head_size)
     keys = key_cache.reshape(blocks_here, block_len, heads, head_size)
     values = value_cache.reshape(blocks_here, block_len, heads, head_size)

time: 96.1 us -> 90.1 us (0.938)
  blocking collectives: 39.5 us -> 24.4 us
  starting transfers between devices: 13.1 us -> 18.1 us
  waiting for transfers between devices: 9.12 us -> 11.7 us
  local copies, waits for them, and re-layouts: 16.7 us -> 18 us
    all_gather x1 -> x0, blocking collectives: 15.1 us -> none  [local(): whole_query = lax.all_gather(query, 'seq', axis=0, tiled=True)]
    all_to_all x0 -> x1, starting transfers between devices: none -> 6.35 us  [local(): lax.all_to_all(jnp.stack([query] * lax.axis_size('seq')), 'seq', 0, 0)]
    all_to_all x1, waiting for transfers between devices: 0.01 us -> 1.7 us  [local(): lax.all_to_all(local_top[None], 'seq', split_axis=1, concat_axis=0, tiled...]
    all_to_all x1, starting transfers between devices: 5.09 us -> 3.4 us  [local(): lax.all_to_all(local_total[None], 'seq', split_axis=1, concat_axis=0, til...]
    another operation x0 -> x1, local copies, waits for them, and re-layouts: none -> 1.32 us  [local(): jnp.stack([query] * lax.axis_size('seq'))]
    unnamed x11 -> x10, local copies, waits for them, and re-layouts: 12.6 us -> 12.6 us
  transfers between devices with their start and end apart: 3 -> 4, of which waited for: 2 -> 3; matrix products, arithmetic and copies ran while one was open for 13% -> 24% of each run, Pallas kernels for 0% -> 0%
where the time goes in v1:
time: 90.1 us; the launch traced here: 89.2 us
  blocking collectives  24.4 us (27%)
  starting transfers between devices  18.1 us (20%)
  local copies, waits for them, and re-layouts  18 us (20%)
  matrix products  12.5 us (14%)
  waiting for transfers between devices  11.7 us (13%)
  other arithmetic  3.76 us (4%)
    all_gather x1, blocking collectives, local(): attention = lax.all_gather(mine, 'seq', axis=0, tiled=True)  13.2 us
    unnamed x10, local copies, waits for them, and re-layouts  12.6 us
    unnamed x1, blocking collectives  11.3 us
    dot_general x1, matrix products, local(): jnp.dot(attention, out_weight, preferred_element_type=jnp.float32)  6.41 us
    all_to_all x1, starting transfers between devices, local(): lax.all_to_all(jnp.stack([query] * lax.axis_size('seq')), 'seq', 0, 0)  6.35 us
    all_to_all x1, waiting for transfers between devices, local(): lax.all_to_all(local_acc[None], 'seq', split_axis=1, concat_axis=0, tiled...  5.46 us
    all_to_all x1, starting transfers between devices, local(): lax.all_to_all(local_top[None], 'seq', split_axis=1, concat_axis=0, tiled...  5.09 us
    all_to_all x1, waiting for transfers between devices, local(): lax.all_to_all(local_total[None], 'seq', split_axis=1, concat_axis=0, til...  4.5 us
  transfers between devices with their start and end apart: 4, of which 3 were waited for; matrix products, arithmetic and copies ran while one was open for 24% of the time, Pallas kernels for 0%

profile of v1, /device:TPU:0, one launch (start us, length us, event | category | flops | bytes accessed | tf_op | source)
XLA Modules:
  0.0 89.2 jit_solution(8895309502956765347)
XLA Ops:
  0.0 1.3 %stack.2 = bf16[4,2,1792]{2,1,0:T(2,128)(2,1)} broadcast(bf16[2,1792]{1,0:T(2,128)(2,1)} %param.8), dimensions={1,2} | broadcast | bytes 35840 | tf_op jit(solution)/shard_map/stack | solution.py:17
  1.3 6.3 %all-to-all-start = ((bf16[4,2,1792]{2,1,0:T(2,128)(2,1)}), bf16[4,2,1792]{2,1,0:T(2,128)(2,1)S(1)}, u32[]{:S(2)}, u32[]{:S(2)}) async-start(bf16[4,2,1792]{2,1,0:T(2,128)(2,1)} %stack.2), calls=%async_computation | async-start | bytes 57344 | tf_op jit(solution)/shard_map/all_to_all | solution.py:17
  7.7 0.7 compare_select_fusion
  8.3 0.7 compare_and_fusion
  9.0 0.6 gather_fusion
  9.7 0.7 broadcast_add_fusion
  10.5 0.7 iota_compare_fusion
  11.2 6.0 %copy.49 = bf16[4,256,1792]{1,2,0:T(8,128)(2,1)} copy(bf16[4,256,1792]{2,1,0:T(8,128)(2,1)} %param.9) | data formatting | bytes 7340032 | tf_op args[1]
  17.2 6.0 %copy.50 = bf16[4,256,1792]{1,2,0:T(8,128)(2,1)} copy(bf16[4,256,1792]{2,1,0:T(8,128)(2,1)} %param.10) | data formatting | bytes 7340032 | tf_op args[2]
  25.1 2.6 %fusion.9 = f32[4,14,1,256]{3,2,1,0:T(1,128)S(1)} fusion(bf16[4,256,14,128]{1,3,2,0:T(8,128)(2,1)} %bitcast.33, bf16[4,14,128,1]{2,1,0,3:T(8,128)(2,1)S(1)} %select_bitcast_fusion), kind=kOutput, calls=%fused_computation.16 | convolution fusion | flops 3670016 | bytes 3741696 | tf_op jit(solution)/shard_map/bthd,bhd->bht/dot_general | solution.py:23
  28.2 0.7 copy.54
  28.8 5.1 %all-to-all-start.2 = ((f32[1,8,14]{2,0,1:T(1,128)}), f32[1,8,14]{2,0,1:T(1,128)S(1)}, u32[]{:S(2)}, u32[]{:S(2)}) async-start(f32[1,8,14]{2,0,1:T(1,128)} %copy.54), calls=%async_computation.2 | async-start | bytes 8192 | tf_op jit(solution)/shard_map/all_to_all | solution.py:44
  33.9 3.1 %fusion.2 = f32[4,14,1,128]{3,2,1,0:T(1,128)S(1)} fusion(bf16[4,256,14,128]{1,3,2,0:T(8,128)(2,1)} %bitcast.32, bf16[4,14,256,1]{2,0,1,3:T(4,128)(2,1)S(1)} %get-tuple-element.10), kind=kOutput, calls=%fused_computation.6 | convolution fusion | flops 3670016 | bytes 3727360 | tf_op jit(solution)/shard_map/bht,bthd->bhd/dot_general | solution.py:34
  37.1 0.7 copy.57
  37.8 1.7 %all-to-all-done.2 = f32[1,8,14]{2,0,1:T(1,128)S(1)} async-done(((f32[1,8,14]{2,0,1:T(1,128)}), f32[1,8,14]{2,0,1:T(1,128)S(1)}, u32[]{:S(2)}, u32[]{:S(2)}) %all-to-all-start.2) | async-done | bytes 480 | tf_op jit(solution)/shard_map/all_to_all | solution.py:44
  39.5 3.4 %all-to-all-start.3 = ((f32[1,8,14]{2,0,1:T(1,128)}), f32[1,8,14]{2,0,1:T(1,128)S(1)}, u32[]{:S(2)}, u32[]{:S(2)}) async-start(f32[1,8,14]{2,0,1:T(1,128)} %copy.57), calls=%async_computation.3 | async-start | bytes 8192 | tf_op jit(solution)/shard_map/all_to_all | solution.py:45
  43.3 0.7 copy.51
  44.0 4.5 %all-to-all-done.3 = f32[1,8,14]{2,0,1:T(1,128)S(1)} async-done(((f32[1,8,14]{2,0,1:T(1,128)}), f32[1,8,14]{2,0,1:T(1,128)S(1)}, u32[]{:S(2)}, u32[]{:S(2)}) %all-to-all-start.3) | async-done | bytes 480 | tf_op jit(solution)/shard_map/all_to_all | solution.py:45
  48.5 3.3 %all-to-all-start.1 = ((f32[1,8,14,128]{3,0,2,1:T(1,128)}), f32[1,8,14,128]{3,0,2,1:T(1,128)S(1)}, u32[]{:S(2)}, u32[]{:S(2)}) async-start(f32[1,8,14,128]{3,0,2,1:T(1,128)} %copy.51), calls=%async_computation.1 | async-start | bytes 114688 | tf_op jit(solution)/shard_map/all_to_all | solution.py:46
  52.0 5.5 %all-to-all-done.1 = f32[1,8,14,128]{3,0,2,1:T(1,128)S(1)} async-done(((f32[1,8,14,128]{3,0,2,1:T(1,128)}), f32[1,8,14,128]{3,0,2,1:T(1,128)S(1)}, u32[]{:S(2)}, u32[]{:S(2)}) %all-to-all-start.1) | async-done | bytes 57376 | tf_op jit(solution)/shard_map/all_to_all | solution.py:46
  57.7 13.2 %all-gather = bf16[4,2,1792]{2,1,0:T(2,128)(2,1)S(1)} all-gather(bf16[1,2,1792]{2,1,0:T(2,128)(2,1)S(1)} %fusion.15), channel_id=1, replica_groups=mesh['group'=2,'seq'=4,'tensor'=4] {'seq'}, dimensions={0}, use_global_device_ids=true | all-gather | bytes 35840 | tf_op jit(solution)/shard_map/all_gather | solution.py:57
  70.9 6.4 %fusion.20 = f32[8,3584]{1,0:T(8,128)S(1)} fusion(bf16[8,1792]{1,0:T(8,128)(2,1)S(1)} %reshape.156, bf16[1792,3584]{1,0:T(8,128)(2,1)} %param.15), kind=kOutput, calls=%fused_computation.41 | convolution fusion | flops 102760448 | bytes 12988416 | tf_op jit(solution)/shard_map/dot_general | solution.py:59
  77.3 11.3 %all-reduce = bf16[8,3584]{1,0:T(8,128)(2,1)S(1)} all-reduce(f32[8,3584]{1,0:T(8,128)S(1)} %fusion.20), channel_id=2, replica_groups=mesh['group'=2,'seq'=4,'tensor'=4] {'tensor'}, use_global_device_ids=true, to_apply=%region_7.8.clone | all-reduce | flops 28672 | bytes 172032
  88.6 0.6 dynamic-slice_convert_fusion
  (28 shorter events, 2.9 us)
Async XLA Ops:
  0.0 9.0 %copy-start = (s32[8]{0:T(128)S(1)}, s32[8]{0:T(128)}, u32[]{:S(2)}) copy-start(s32[8]{0:T(128)} %param.14) | copy-start | bytes 100
  1.3 23.1 %all-to-all-start = ((bf16[4,2,1792]{2,1,0:T(2,128)(2,1)}), bf16[4,2,1792]{2,1,0:T(2,128)(2,1)S(1)}, u32[]{:S(2)}, u32[]{:S(2)}) async-start(bf16[4,2,1792]{2,1,0:T(2,128)(2,1)} %stack.2), calls=%async_computation | async-start | bytes 57344 | tf_op jit(solution)/shard_map/all_to_all | solution.py:17
  17.2 6.0 %copy-start.2 = (u32[32]{0:T(128)S(1)}, u32[32]{0:T(128)}, u32[]{:S(2)}) copy-start(u32[32]{0:T(128)} %constant.39) | copy-start | bytes 388
  23.2 4.6 %copy-start.1 = (f32[14]{0:T(128)S(1)}, f32[14]{0:T(128)}, u32[]{:S(2)}) copy-start(f32[14]{0:T(128)} %param.11) | copy-start | bytes 172
  28.8 10.7 %all-to-all-start.2 = ((f32[1,8,14]{2,0,1:T(1,128)}), f32[1,8,14]{2,0,1:T(1,128)S(1)}, u32[]{:S(2)}, u32[]{:S(2)}) async-start(f32[1,8,14]{2,0,1:T(1,128)} %copy.54), calls=%async_computation.2 | async-start | bytes 8192 | tf_op jit(solution)/shard_map/all_to_all | solution.py:44
  39.5 9.0 %all-to-all-start.3 = ((f32[1,8,14]{2,0,1:T(1,128)}), f32[1,8,14]{2,0,1:T(1,128)S(1)}, u32[]{:S(2)}, u32[]{:S(2)}) async-start(f32[1,8,14]{2,0,1:T(1,128)} %copy.57), calls=%async_computation.3 | async-start | bytes 8192 | tf_op jit(solution)/shard_map/all_to_all | solution.py:45
  48.5 9.0 %all-to-all-start.1 = ((f32[1,8,14,128]{3,0,2,1:T(1,128)}), f32[1,8,14,128]{3,0,2,1:T(1,128)S(1)}, u32[]{:S(2)}, u32[]{:S(2)}) async-start(f32[1,8,14,128]{3,0,2,1:T(1,128)} %copy.51), calls=%async_computation.1 | async-start | bytes 114688 | tf_op jit(solution)/shard_map/all_to_all | solution.py:46
